TPU v7x, 32 devices: a whole 2x2x4 slice. The times are simulated.
32 devices in a mesh: gx: 2 (over y), gy: 4 (over z), gz: 4 (over x, core).
Axes of the slice: x: 2, y: 2, z: 4, core: 2. Of those that a mesh axis runs over, the one named last changes fastest.
Arguments:
- section: float32 [25, 8, 64, 256], P(None, 'gz', 'gy', 'gx'), may hold values from -0.4 to 1.4, as said below
- base: float32 [25, 8, 64, 256], P(None, 'gz', 'gy', 'gx'), may hold values from -0.4 to 1.4, as said below
- accum: float32 [25, 8, 64, 256], P(None, 'gz', 'gy', 'gx'), may hold values from -4 to 4
Outputs:
- next_section: float32 [25, 8, 64, 256], P(None, 'gz', 'gy', 'gx')
- next_accum: float32 [25, 8, 64, 256], P(None, 'gz', 'gy', 'gx')
- slab: float32 [25, 8, 64, 256], P(None, 'gz')
Inputs may be any that keep to these rules, and one draw needn't show every extreme that they name: `section`: fields 0 and 17 (conformal factor and lapse) lie in 0.6 to 1.4; fields 1, 4 and 6 (the metric's diagonal) lie within 0.4 of 1; all other fields lie within 0.4 of 0. `base`: fields 0 and 17 (conformal factor and lapse) lie in 0.6 to 1.4; fields 1, 4 and 6 (the metric's diagonal) lie within 0.4 of 1; all other fields lie within 0.4 of 0.
All inputs are finite; a program needn't handle non-finite values.
Results may differ from a plain program's by a relative error of at most 0.0003.
Values sent between devices are 32-bit elements; how exact they have to be, the bound alone decides.
A program may use at most 64 MiB of HBM per device.

v0:
```python
import jax
import jax.numpy as jnp
from jax import lax
from jax.sharding import PartitionSpec as P

STEP_DT = 0.25
SPACING = 1.0
DISSIPATE = 0.1
DRIVER_ETA = 2.0
KAPPA_ONE = 0.1
FIRST_TAPS = (1.0 / 12.0, -8.0 / 12.0, 0.0, 8.0 / 12.0, -1.0 / 12.0)
SECOND_TAPS = (-1.0 / 12.0, 16.0 / 12.0, -30.0 / 12.0, 16.0 / 12.0, -1.0 / 12.0)
FOURTH_TAPS = (1.0, -4.0, 6.0, -4.0, 1.0)
PAIR_SLOT = ((0, 1, 2), (1, 3, 4), (2, 4, 5))
PAIR_LIST = ((0, 0), (0, 1), (0, 2), (1, 1), (1, 2), (2, 2))


def extended(block, sides, width):
    for axis, dim in sides:
        count = lax.axis_size(axis)
        forward = [(i, i + 1) for i in range(count - 1)]
        forward.append((count - 1, 0))
        backward = [(target, source) for source, target in forward]
        low = lax.ppermute(
            lax.slice_in_dim(block, block.shape[dim] - width, None, axis=dim), axis, forward
        )
        high = lax.ppermute(lax.slice_in_dim(block, 0, width, axis=dim), axis, backward)
        block = jnp.concatenate([low, block, high], axis=dim)
    return block


def window(padded, shifts):
    interior = (padded.shape[1] - 4, padded.shape[2] - 4, padded.shape[3] - 4)
    corner = (2 + shifts[2], 2 + shifts[1], 2 + shifts[0])
    return padded[
        :,
        corner[0] : corner[0] + interior[0],
        corner[1] : corner[1] + interior[1],
        corner[2] : corner[2] + interior[2],
    ]


def moved(direction, amount):
    shifts = [0, 0, 0]
    shifts[direction] = amount
    return shifts


def line_sum(padded, direction, weights):
    running = None
    for position in range(5):
        if weights[position] != 0.0:
            weighted = weights[position] * window(padded, moved(direction, position - 2))
            running = weighted if running is None else running + weighted
    return running


def cross_sum(padded, first_dir, second_dir):
    running = None
    for first_pos in range(5):
        for second_pos in range(5):
            factor = FIRST_TAPS[first_pos] * FIRST_TAPS[second_pos]
            if factor != 0.0:
                shifts = [0, 0, 0]
                shifts[first_dir] = first_pos - 2
                shifts[second_dir] = second_pos - 2
                weighted = factor * window(padded, shifts)
                running = weighted if running is None else running + weighted
    return running


def evolve_rate(padded):
    centre = window(padded, (0, 0, 0))
    gradients = [line_sum(padded, direction, FIRST_TAPS) / SPACING for direction in range(3)]
    curves = [
        line_sum(padded, direction, SECOND_TAPS) / (SPACING * SPACING) for direction in range(3)
    ]
    smoothing = (
        line_sum(padded, 0, FOURTH_TAPS)
        + line_sum(padded, 1, FOURTH_TAPS)
        + line_sum(padded, 2, FOURTH_TAPS)
    )
    chosen = jnp.concatenate([padded[0:1], padded[17:21]], axis=0)
    mixed_terms = {}
    for dir_pair in ((0, 1), (0, 2), (1, 2)):
        mixed_terms[dir_pair] = cross_sum(chosen, dir_pair[0], dir_pair[1]) / (SPACING * SPACING)

    def second_of(chosen_slot, field_slot, axis_one, axis_two):
        if axis_one == axis_two:
            return curves[axis_one][field_slot]
        return mixed_terms[min(axis_one, axis_two), max(axis_one, axis_two)][chosen_slot]

    def metric_of(axis_one, axis_two):
        return centre[1 + PAIR_SLOT[axis_one][axis_two]]

    def traceless_of(axis_one, axis_two):
        return centre[8 + PAIR_SLOT[axis_one][axis_two]]

    def inverse_of(axis_one, axis_two):
        return (2.0 if axis_one == axis_two else 0.0) - metric_of(axis_one, axis_two)

    def advect(field_slot):
        return (
            centre[18] * gradients[0][field_slot]
            + centre[19] * gradients[1][field_slot]
            + centre[20] * gradients[2][field_slot]
        )

    conformal = centre[0]
    trace_curv = centre[7]
    lapse_field = centre[17]
    theta_field = centre[24]
    divergence = gradients[0][18] + gradients[1][19] + gradients[2][20]
    lap_conformal = curves[0][0] + curves[1][0] + curves[2][0]
    squares_a = sum(
        (traceless_of(axis_one, axis_two) ** 2 for axis_one in range(3) for axis_two in range(3))
    )

    def lapse_dd(axis_one, axis_two):
        return second_of(1, 17, axis_one, axis_two)

    ricci_table = []
    for axis_one, axis_two in PAIR_LIST:
        field_slot = 1 + PAIR_SLOT[axis_one][axis_two]
        flat_part = curves[0][field_slot] + curves[1][field_slot] + curves[2][field_slot]
        conformal_part = second_of(0, 0, axis_one, axis_two) + (
            lap_conformal if axis_one == axis_two else 0.0
        )
        ricci_table.append(
            -0.5 * flat_part
            + 0.5 * (gradients[axis_one][14 + axis_two] + gradients[axis_two][14 + axis_one])
            + conformal_part / (2.0 * conformal)
        )

    def ricci_of(axis_one, axis_two):
        return ricci_table[PAIR_SLOT[axis_one][axis_two]]

    ricci_scalar = conformal * sum(
        (
            inverse_of(axis_one, axis_two) * ricci_of(axis_one, axis_two)
            for axis_one in range(3)
            for axis_two in range(3)
        )
    )
    lapse_trace = sum(
        (
            inverse_of(axis_one, axis_two) * lapse_dd(axis_one, axis_two)
            for axis_one in range(3)
            for axis_two in range(3)
        )
    )
    rates = [None] * 25
    rates[0] = advect(0) + 2.0 / 3.0 * conformal * (lapse_field * trace_curv - divergence)
    for axis_one, axis_two in PAIR_LIST:
        field_slot = PAIR_SLOT[axis_one][axis_two]
        lie_part = sum(
            (
                metric_of(axis_one, axis_sum) * gradients[axis_two][18 + axis_sum]
                + metric_of(axis_two, axis_sum) * gradients[axis_one][18 + axis_sum]
                for axis_sum in range(3)
            )
        )
        rates[1 + field_slot] = (
            advect(1 + field_slot)
            - 2.0 * lapse_field * traceless_of(axis_one, axis_two)
            + lie_part
            - 2.0 / 3.0 * metric_of(axis_one, axis_two) * divergence
        )
    rates[7] = (
        advect(7)
        - conformal * lapse_trace
        + lapse_field * (squares_a + trace_curv * trace_curv / 3.0)
        + KAPPA_ONE * lapse_field * theta_field
    )

    def source_of(axis_one, axis_two):
        return -lapse_dd(axis_one, axis_two) + lapse_field * ricci_of(axis_one, axis_two)

    trace_part = sum(
        (
            inverse_of(axis_one, axis_two) * source_of(axis_one, axis_two)
            for axis_one in range(3)
            for axis_two in range(3)
        )
    )
    for axis_one, axis_two in PAIR_LIST:
        field_slot = PAIR_SLOT[axis_one][axis_two]
        free_part = source_of(axis_one, axis_two) - metric_of(axis_one, axis_two) * trace_part / 3.0
        product_part = sum(
            (
                traceless_of(axis_one, axis_sum) * traceless_of(axis_sum, axis_two)
                for axis_sum in range(3)
            )
        )
        lie_part = sum(
            (
                traceless_of(axis_one, axis_sum) * gradients[axis_two][18 + axis_sum]
                + traceless_of(axis_two, axis_sum) * gradients[axis_one][18 + axis_sum]
                for axis_sum in range(3)
            )
        )
        rates[8 + field_slot] = (
            advect(8 + field_slot)
            + conformal * free_part
            + lapse_field * (trace_curv * traceless_of(axis_one, axis_two) - 2.0 * product_part)
            + lie_part
            - 2.0 / 3.0 * traceless_of(axis_one, axis_two) * divergence
        )
    for axis_one in range(3):
        gauge_part = (
            -2.0
            * sum(
                (
                    traceless_of(axis_one, axis_two) * gradients[axis_two][17]
                    for axis_two in range(3)
                )
            )
            + 2.0
            * lapse_field
            * (
                -(2.0 / 3.0)
                * sum(
                    (
                        inverse_of(axis_one, axis_two) * gradients[axis_two][7]
                        for axis_two in range(3)
                    )
                )
                - 1.5
                * sum(
                    (
                        traceless_of(axis_one, axis_two) * gradients[axis_two][0]
                        for axis_two in range(3)
                    )
                )
                / conformal
            )
            + curves[0][18 + axis_one]
            + curves[1][18 + axis_one]
            + curves[2][18 + axis_one]
            + sum(
                (
                    second_of(2 + axis_two, 18 + axis_two, axis_one, axis_two)
                    for axis_two in range(3)
                )
            )
            / 3.0
            + 2.0 / 3.0 * centre[14 + axis_one] * divergence
            - sum(
                (
                    centre[14 + axis_two] * gradients[axis_two][18 + axis_one]
                    for axis_two in range(3)
                )
            )
        )
        rates[14 + axis_one] = advect(14 + axis_one) + gauge_part
        rates[18 + axis_one] = advect(18 + axis_one) + 0.75 * centre[21 + axis_one]
        rates[21 + axis_one] = (
            advect(21 + axis_one) + gauge_part - DRIVER_ETA * centre[21 + axis_one]
        )
    rates[17] = advect(17) - 2.0 * lapse_field * (trace_curv - 2.0 * theta_field)
    rates[24] = (
        advect(24)
        + 0.5 * lapse_field * (ricci_scalar + 2.0 / 3.0 * trace_curv * trace_curv - squares_a)
        - 2.0 * KAPPA_ONE * lapse_field * theta_field
    )
    return jnp.stack(rates, axis=0) + -DISSIPATE / 16.0 * smoothing


def shards(section, base, accum):
    padded = extended(section, (("gx", 3), ("gy", 2), ("gz", 1)), 2)
    rates = evolve_rate(padded)
    next_section = base + 0.5 * STEP_DT * rates
    next_accum = accum + STEP_DT / 3.0 * rates
    stacked = lax.all_gather(next_section[None], ("gx", "gy"), axis=0, tiled=True)
    width_parts = lax.axis_size("gx")
    height_parts = lax.axis_size("gy")
    fields_count, planes, block_rows, block_cols = next_section.shape
    regrouped = stacked.reshape(
        width_parts, height_parts, fields_count, planes, block_rows, block_cols
    )
    regrouped = jnp.transpose(regrouped, (2, 3, 1, 4, 0, 5))
    slab = regrouped.reshape(
        fields_count, planes, height_parts * block_rows, width_parts * block_cols
    )
    return (next_section, next_accum, slab)


def solution(mesh):
    return jax.shard_map(
        shards,
        mesh=mesh,
        in_specs=(P(None, "gz", "gy", "gx"), P(None, "gz", "gy", "gx"), P(None, "gz", "gy", "gx")),
        out_specs=(P(None, "gz", "gy", "gx"), P(None, "gz", "gy", "gx"), P(None, "gz", None, None)),
        check_vma=False,
    )
```

profile of v0, /device:TPU:0, one launch (start us, length us, event | category | flops | bytes accessed | tf_op | source)
XLA Modules:
  0.0 147.6 jit_solution(17739770399020548956)
XLA Ops:
  7.2 0.0 copy-start
  7.2 0.0 all-gather.3.cloned.1.call-start
  7.2 1.3 fusion.195
  8.6 3.1 %collective-permute-start = (f32[25,2,16,2]{3,2,1,0:T(8,128)S(1)}, f32[25,2,16,2]{3,2,1,0:T(8,128)S(1)}, u32[]{:S(2)}, u32[]{:S(2)}) collective-permute-start(f32[25,2,16,2]{3,2,1,0:T(8,128)S(1)} %get-tuple-element.39), channel_id=1, source_target_pairs={{0,16},{16,0},{1,17},{17,1},{2,18},{18,2},{3,19},{19,3},{4,20},{20... | collective-permute-start | bytes 19208 | tf_op jit(solution)/shard_map/ppermute | solution.py:24
  11.6 0.1 collective-permute-start.1
  11.7 10.2 %collective-permute-done = f32[25,2,16,2]{3,2,1,0:T(8,128)S(1)} collective-permute-done((f32[25,2,16,2]{3,2,1,0:T(8,128)S(1)}, f32[25,2,16,2]{3,2,1,0:T(8,128)S(1)}, u32[]{:S(2)}, u32[]{:S(2)}) %collective-permute-start) | collective-permute-done | bytes 6432 | tf_op jit(solution)/shard_map/ppermute | solution.py:24
  21.9 7.9 %collective-permute-done.1 = f32[25,2,16,2]{3,2,1,0:T(8,128)S(1)} collective-permute-done((f32[25,2,16,2]{3,2,1,0:T(8,128)S(1)}, f32[25,2,16,2]{3,2,1,0:T(8,128)S(1)}, u32[]{:S(2)}, u32[]{:S(2)}) %collective-permute-start.1) | collective-permute-done | bytes 6432 | tf_op jit(solution)/shard_map/ppermute | solution.py:27
  29.9 0.0 copy-done
  29.9 0.4 pad_maximum_fusion.22
  30.3 1.8 %collective-permute-start.2 = (f32[25,2,2,132]{3,2,1,0:T(2,128)S(1)}, f32[25,2,2,132]{3,2,1,0:T(2,128)S(1)}, u32[]{:S(2)}, u32[]{:S(2)}) collective-permute-start(f32[25,2,2,132]{3,2,1,0:T(2,128)S(1)} %get-tuple-element.36), channel_id=1, source_target_pairs={{0,4},{4,8},{8,12},{12,0},{1,5},{5,9},{9,13},{13,1},{2,6},{6,10},{... | collective-permute-start | bytes 158408 | tf_op jit(solution)/shard_map/ppermute | solution.py:24
  32.1 2.1 %collective-permute-start.3 = (f32[25,2,2,132]{3,2,1,0:T(2,128)S(1)}, f32[25,2,2,132]{3,2,1,0:T(2,128)S(1)}, u32[]{:S(2)}, u32[]{:S(2)}) collective-permute-start(f32[25,2,2,132]{3,2,1,0:T(2,128)S(1)} %get-tuple-element.37), channel_id=1, source_target_pairs={{4,0},{8,4},{12,8},{0,12},{5,1},{9,5},{13,9},{1,13},{6,2},{10,6},{... | collective-permute-start | bytes 158408 | tf_op jit(solution)/shard_map/ppermute | solution.py:27
  34.2 3.5 %collective-permute-done.2 = f32[25,2,2,132]{3,2,1,0:T(2,128)S(1)} collective-permute-done((f32[25,2,2,132]{3,2,1,0:T(2,128)S(1)}, f32[25,2,2,132]{3,2,1,0:T(2,128)S(1)}, u32[]{:S(2)}, u32[]{:S(2)}) %collective-permute-start.2) | collective-permute-done | bytes 52832 | tf_op jit(solution)/shard_map/ppermute | solution.py:24
  37.7 0.1 collective-permute-done.3
  37.9 0.6 pad_maximum_fusion
  38.4 0.5 copy.46
  39.0 0.1 collective-permute-start.5
  39.0 0.5 collective-permute-start.4
  39.5 0.7 add_add_fusion.1
  40.3 0.2 add_add_fusion.4
  40.4 20.5 %collective-permute-done.5 = f32[25,2,20,132]{3,1,2,0:T(2,128)S(1)} collective-permute-done((f32[25,2,20,132]{3,1,2,0:T(2,128)S(1)}, f32[25,2,20,132]{3,1,2,0:T(2,128)S(1)}, u32[]{:S(2)}, u32[]{:S(2)}) %collective-permute-start.5) | collective-permute-done | bytes 528032 | tf_op jit(solution)/shard_map/ppermute | solution.py:27
  60.9 0.1 copy.50
  61.0 3.0 %collective-permute-done.4 = f32[25,2,20,132]{3,1,2,0:T(2,128)S(1)} collective-permute-done((f32[25,2,20,132]{3,1,2,0:T(2,128)S(1)}, f32[25,2,20,132]{3,1,2,0:T(2,128)S(1)}, u32[]{:S(2)}, u32[]{:S(2)}) %collective-permute-start.4) | collective-permute-done | bytes 528032 | tf_op jit(solution)/shard_map/ppermute | solution.py:24
  64.0 0.1 copy.47
  64.1 0.2 fusion
  64.3 0.3 fusion.35
  64.7 0.4 fusion.20
  65.1 0.3 fusion.50
  65.4 0.6 add_add_fusion
  66.1 0.9 add_add_fusion.2
  67.3 0.1 constant_dynamic-update-slice_fusion.18
  67.6 0.1 constant_dynamic-update-slice_fusion.12
  67.6 0.0 copy-start.1
  67.7 0.1 constant_dynamic-update-slice_fusion.10
  67.9 0.7 copy-done.1
  68.7 0.0 copy-start.2
  68.7 1.6 %multiply_add_fusion = (f32[25,2,16,128]{3,2,1,0:T(8,128)}, f32[25,2,16,128]{3,2,1,0:T(8,128)S(1)}) fusion(f32[25,2,16,128]{3,2,1,0:T(8,128)S(1)} %copy-done.1, f32[25,2,16,128]{3,2,1,0:T(8,128)S(1)} %constant_dynamic-update-slice_fusion.2, f32[25,2,20,132]{3,2,1,0:T(8,128)S(1)} %copy.50, f32[25,2,16,128]{3,2,1,0:T(8,128)S(1)} %get-tuple-element.31, ...), kind=kLoop, calls=%fused_computation.48 | loop fusion | flops 2764800 | bytes 6150400 | tf_op jit(solution)/shard_map/add | solution.py:273
  70.2 0.0 copy-done.2
  70.3 0.8 multiply_add_fusion.1
  71.1 0.0 all-gather.3.cloned.1.call-update
  71.1 61.4 %all-gather.3.cloned.1.call-done = f32[200,2,16,128]{3,2,1,0:T(8,128)} async-done(((f32[25,2,16,128]{3,2,1,0:T(8,128)}), f32[200,2,16,128]{3,2,1,0:T(8,128)}) %all-gather.3.cloned.1.call-update) | async-done | bytes 3276816 | tf_op jit(solution)/shard_map/all_gather | solution.py:274
  132.5 4.5 %copy.54 = f32[25,2,4,16,2,128]{5,4,3,2,1,0:T(2,128)S(1)} copy(f32[25,2,4,16,2,128]{5,3,1,0,2,4:T(8,128)} %bitcast.3) | data formatting | bytes 6553600 | tf_op jit(solution)/shard_map/transpose | solution.py:281
  137.0 3.8 %reshape.13 = f32[25,2,64,256]{3,2,1,0:T(8,128)} reshape(f32[25,2,4,16,2,128]{5,4,3,2,1,0:T(2,128)S(1)} %copy.54) | data formatting | bytes 6553600 | tf_op jit(solution)/shard_map/reshape | solution.py:282
  (23 shorter events, 0.6 us)
Async XLA Ops:
  7.2 22.7 %copy-start = (f32[25,2,16,128]{3,2,1,0:T(8,128)S(1)}, f32[25,2,16,128]{3,2,1,0:T(8,128)}, u32[]{:S(2)}) copy-start(f32[25,2,16,128]{3,2,1,0:T(8,128)} %param.3) | copy-start | bytes 1228804
  7.2 125.3 %all-gather.3.cloned.1.call-start = ((), (), s32[]{:S(2)}) async-start(), calls=%async_computation | async-start | bytes 3686400 | tf_op jit(solution)/shard_map/all_gather | solution.py:274
  8.6 13.4 %collective-permute-start = (f32[25,2,16,2]{3,2,1,0:T(8,128)S(1)}, f32[25,2,16,2]{3,2,1,0:T(8,128)S(1)}, u32[]{:S(2)}, u32[]{:S(2)}) collective-permute-start(f32[25,2,16,2]{3,2,1,0:T(8,128)S(1)} %get-tuple-element.39), channel_id=1, source_target_pairs={{0,16},{16,0},{1,17},{17,1},{2,18},{18,2},{3,19},{19,3},{4,20},{20... | collective-permute-start | bytes 19208 | tf_op jit(solution)/shard_map/ppermute | solution.py:24
  11.6 18.2 %collective-permute-start.1 = (f32[25,2,16,2]{3,2,1,0:T(8,128)S(1)}, f32[25,2,16,2]{3,2,1,0:T(8,128)S(1)}, u32[]{:S(2)}, u32[]{:S(2)}) collective-permute-start(f32[25,2,16,2]{3,2,1,0:T(8,128)S(1)} %get-tuple-element.40), channel_id=1, source_target_pairs={{16,0},{0,16},{17,1},{1,17},{18,2},{2,18},{19,3},{3,19},{20,4},{4,... | collective-permute-start | bytes 19208 | tf_op jit(solution)/shard_map/ppermute | solution.py:27
  30.3 7.5 %collective-permute-start.2 = (f32[25,2,2,132]{3,2,1,0:T(2,128)S(1)}, f32[25,2,2,132]{3,2,1,0:T(2,128)S(1)}, u32[]{:S(2)}, u32[]{:S(2)}) collective-permute-start(f32[25,2,2,132]{3,2,1,0:T(2,128)S(1)} %get-tuple-element.36), channel_id=1, source_target_pairs={{0,4},{4,8},{8,12},{12,0},{1,5},{5,9},{9,13},{13,1},{2,6},{6,10},{... | collective-permute-start | bytes 158408 | tf_op jit(solution)/shard_map/ppermute | solution.py:24
  32.1 5.8 %collective-permute-start.3 = (f32[25,2,2,132]{3,2,1,0:T(2,128)S(1)}, f32[25,2,2,132]{3,2,1,0:T(2,128)S(1)}, u32[]{:S(2)}, u32[]{:S(2)}) collective-permute-start(f32[25,2,2,132]{3,2,1,0:T(2,128)S(1)} %get-tuple-element.37), channel_id=1, source_target_pairs={{4,0},{8,4},{12,8},{0,12},{5,1},{9,5},{13,9},{1,13},{6,2},{10,6},{... | collective-permute-start | bytes 158408 | tf_op jit(solution)/shard_map/ppermute | solution.py:27
  39.0 21.9 %collective-permute-start.5 = (f32[25,2,20,132]{3,1,2,0:T(2,128)S(1)}, f32[25,2,20,132]{3,1,2,0:T(2,128)S(1)}, u32[]{:S(2)}, u32[]{:S(2)}) collective-permute-start(f32[25,2,20,132]{3,1,2,0:T(2,128)S(1)} %copy.46), channel_id=1, source_target_pairs={{1,0},{2,1},{3,2},{0,3},{5,4},{6,5},{7,6},{4,7},{9,8},{10,9},{11,1... | collective-permute-start | bytes 1584008 | tf_op jit(solution)/shard_map/ppermute | solution.py:27
  39.0 25.0 %collective-permute-start.4 = (f32[25,2,20,132]{3,1,2,0:T(2,128)S(1)}, f32[25,2,20,132]{3,1,2,0:T(2,128)S(1)}, u32[]{:S(2)}, u32[]{:S(2)}) collective-permute-start(f32[25,2,20,132]{3,1,2,0:T(2,128)S(1)} %copy.46), channel_id=1, source_target_pairs={{0,1},{1,2},{2,3},{3,0},{4,5},{5,6},{6,7},{7,4},{8,9},{9,10},{10,1... | collective-permute-start | bytes 1584008 | tf_op jit(solution)/shard_map/ppermute | solution.py:24
  67.6 1.0 copy-start.1
  68.7 1.6 %copy-start.2 = (f32[25,2,16,128]{3,2,1,0:T(8,128)S(1)}, f32[25,2,16,128]{3,2,1,0:T(8,128)}, u32[]{:S(2)}) copy-start(f32[25,2,16,128]{3,2,1,0:T(8,128)} %param.4) | copy-start | bytes 1228804
Sparse Core Ops, SparseCore 0:
  71.2 61.2 all-gather.2
where the time goes:
time: 148 us
  waiting for transfers between devices  107 us (72%)
  between operations  14.3 us (10%)
  local copies, waits for them, and re-layouts  11.2 us (8%)
  other arithmetic  7.84 us (5%)
  starting transfers between devices  7.67 us (5%)
    all_gather x1, waiting for transfers between devices, shards(): lax.all_gather(next_section[None], ('gx', 'gy'), axis=0, tiled=True)  61.4 us
    ppermute x3, waiting for transfers between devices, extended(): lax.ppermute(lax.slice_in_dim(block, 0, width, axis=dim), axis, backward)  28.5 us
    ppermute x3, waiting for transfers between devices, extended(): lax.ppermute(lax.slice_in_dim(block, block.shape[dim] - width, None, axis...  16.7 us
    ppermute x3, starting transfers between devices, extended(): lax.ppermute(lax.slice_in_dim(block, block.shape[dim] - width, None, axis...  5.41 us
    transpose x1, local copies, waits for them, and re-layouts, shards(): regrouped = jnp.transpose(regrouped, (2, 3, 1, 4, 0, 5))  4.46 us
    reshape x1, local copies, waits for them, and re-layouts, shards(): regrouped.reshape(fields_count, planes, height_parts * block_rows, width_...  3.82 us
  transfers between devices with their start and end apart: 7, of which 7 were waited for; matrix products, arithmetic and copies ran while one was open for 1% of the time, Pallas kernels for 0%

commit v1 on v0

v1 whole, which is shorter than its diff:
```python
import functools

import jax
import jax.numpy as jnp
from jax import lax
from jax.experimental import pallas as pl
from jax.experimental.pallas import tpu as pltpu
from jax.sharding import PartitionSpec as P

STEP_DT = 0.25
DISSIPATE = 0.1
DRIVER_ETA = 2.0
KAPPA_ONE = 0.1
PAIR_SLOT = ((0, 1, 2), (1, 3, 4), (2, 4, 5))
PAIR_LIST = ((0, 0), (0, 1), (0, 2), (1, 1), (1, 2), (2, 2))
MESH = pl.DeviceIdType.MESH
MIXED = (0, 17, 18, 19, 20)
MIXED_RUNS = ((0, 1), (17, 4))
PAD = 8


def first_of(m2, m1, p1, p2):
    return (8.0 / 12.0) * (p1 - m1) - (1.0 / 12.0) * (p2 - m2)


def rates_of_plane(plane, rows, lanes, xb, tb, emit):
    lane = lax.broadcasted_iota(jnp.int32, (rows, lanes), 1)
    quad = lane & 3
    edge_one = (lane < 1) | (lane >= lanes - 1)
    edge_two = (lane < 2) | (lane >= lanes - 2)

    def cell(field, dz=0, dy=0):
        return xb[field, plane + 2 + dz, PAD + dy : PAD + dy + rows, :]

    def strip(dz=0, dy=0):
        def side(slot):
            return tb[slot, plane + 2 + dz, PAD + dy : PAD + dy + rows, :]

        if tb.shape[0] == 1:
            return side(0)
        return jnp.where(quad < 2, side(1), side(0))

    def inner(edge):
        return jnp.where(
            quad == 1, pltpu.roll(edge, 1, 1), pltpu.roll(edge, lanes - 1, 1)
        )

    def x_line(field, value, edge, edge_in):
        turn = (lanes - 2 - 4 * field) % lanes
        two = pltpu.roll(edge, turn, 1)
        one = pltpu.roll(edge_in, turn, 1)
        m2 = jnp.where(edge_two & (lane < 64), two, pltpu.roll(value, 2, 1))
        m1 = jnp.where(edge_one & (lane < 64), one, pltpu.roll(value, 1, 1))
        p1 = jnp.where(edge_one & (lane >= 64), one, pltpu.roll(value, lanes - 1, 1))
        p2 = jnp.where(edge_two & (lane >= 64), two, pltpu.roll(value, lanes - 2, 1))
        return m2, m1, p1, p2

    def y_line(read):
        return tuple(read(0, dy) for dy in (-2, -1, 1, 2))

    def z_line(read):
        return tuple(read(dz, 0) for dz in (-2, -1, 1, 2))

    edge = strip()
    edge_in = inner(edge)
    edge_y = first_of(*y_line(strip))
    edge_y_in = inner(edge_y)
    edge_z = first_of(*z_line(strip))
    edge_z_in = inner(edge_z)

    centre, grad, curve, lap, smooth, mixed = {}, {}, {}, {}, {}, {}
    need_lap = (0, 1, 2, 3, 4, 5, 6, 17, 18, 19, 20)
    shift = [cell(18), cell(19), cell(20)]
    advected = {}
    for field in range(25):
        value = cell(field)
        read = functools.partial(cell, field)
        lines = [x_line(field, value, edge, edge_in), y_line(read), z_line(read)]
        near = [m1 + p1 for _, m1, p1, _ in lines]
        far = [m2 + p2 for m2, _, _, p2 in lines]
        near_sum = near[0] + near[1] + near[2]
        far_sum = far[0] + far[1] + far[2]
        smooth = far_sum - 4.0 * near_sum + 18.0 * value
        grads = [first_of(*line) for line in lines]
        centre[field] = value
        grad[field] = grads
        advected[field] = (
            shift[0] * grads[0] + shift[1] * grads[1] + shift[2] * grads[2]
            - (DISSIPATE / 16.0) * smooth
        )
        if field in need_lap:
            lap[field] = (16.0 / 12.0) * near_sum - (1.0 / 12.0) * far_sum - 7.5 * value
        if field in MIXED:
            for axis in range(3):
                if field in (0, 17) or field == 18 + axis:
                    curve[field, axis] = (
                        (16.0 / 12.0) * near[axis] - (1.0 / 12.0) * far[axis] - 2.5 * value
                    )
            if field != 20:
                mixed[field, 0, 1] = first_of(*x_line(field, grads[1], edge_y, edge_y_in))
            if field != 19:
                mixed[field, 0, 2] = first_of(*x_line(field, grads[2], edge_z, edge_z_in))
            if field != 18:
                mixed[field, 1, 2] = first_of(
                    *(
                        first_of(*(cell(field, dz, dy) for dy in (-2, -1, 1, 2)))
                        for dz in (-2, -1, 1, 2)
                    )
                )

    def second(field, one, two):
        if one == two:
            return curve[field, one]
        return mixed[field, min(one, two), max(one, two)]

    def sym(table, one, two):
        return table[PAIR_SLOT[one][two]]

    metric = [centre[1 + k] for k in range(6)]
    traceless = [centre[8 + k] for k in range(6)]
    inverse = [
        (2.0 - metric[k]) if one == two else -metric[k]
        for k, (one, two) in enumerate(PAIR_LIST)
    ]
    count = [1.0 if one == two else 2.0 for one, two in PAIR_LIST]

    def contract(left, right):
        diag = left[0] * right[0] + left[3] * right[3] + left[5] * right[5]
        off = left[1] * right[1] + left[2] * right[2] + left[4] * right[4]
        return diag + 2.0 * off

    chi, trace, lapse, theta = centre[0], centre[7], centre[17], centre[24]
    div = grad[18][0] + grad[19][1] + grad[20][2]
    third_div = (2.0 / 3.0) * div
    squares = contract(traceless, traceless)
    over_chi = 1.0 / chi
    half_over = 0.5 * over_chi
    lapse_dd = [second(17, one, two) for one, two in PAIR_LIST]
    ricci = []
    for k, (one, two) in enumerate(PAIR_LIST):
        conf = second(0, one, two)
        if one == two:
            conf = conf + lap[0]
            grads_g = grad[14 + one][one]
        else:
            grads_g = 0.5 * (grad[14 + two][one] + grad[14 + one][two])
        ricci.append(-0.5 * lap[1 + k] + grads_g + conf * half_over)
    ricci_trace = contract(inverse, ricci)
    lapse_trace = contract(inverse, lapse_dd)
    source_trace = lapse * ricci_trace - lapse_trace

    emit(0, advected[0] + (2.0 / 3.0) * chi * (lapse * trace) - chi * third_div)

    def lie_of(table, one, two):
        total = None
        for k in range(3):
            if one == two:
                term = 2.0 * (sym(table, one, k) * grad[18 + k][one])
            else:
                term = (
                    sym(table, one, k) * grad[18 + k][two]
                    + sym(table, two, k) * grad[18 + k][one]
                )
            total = term if total is None else total + term
        return total

    for k, (one, two) in enumerate(PAIR_LIST):
        emit(
            1 + k,
            advected[1 + k]
            - 2.0 * lapse * traceless[k]
            + lie_of(metric, one, two)
            - metric[k] * third_div,
        )
    emit(
        7,
        advected[7]
        - chi * lapse_trace
        + lapse * (squares + trace * trace * (1.0 / 3.0))
        + KAPPA_ONE * lapse * theta,
    )
    third_trace = source_trace * (1.0 / 3.0)
    for k, (one, two) in enumerate(PAIR_LIST):
        free = lapse * ricci[k] - lapse_dd[k] - metric[k] * third_trace
        product = sum(
            sym(traceless, one, m) * sym(traceless, m, two) for m in range(3)
        )
        emit(
            8 + k,
            advected[8 + k]
            + chi * free
            + lapse * (trace * traceless[k] - 2.0 * product)
            + lie_of(traceless, one, two)
            - traceless[k] * third_div,
        )
    gauges = []
    for one in range(3):
        a_lapse = sum(sym(traceless, one, k) * grad[17][k] for k in range(3))
        a_chi = sum(sym(traceless, one, k) * grad[0][k] for k in range(3))
        g_trace = sum(sym(inverse, one, k) * grad[7][k] for k in range(3))
        b_mixed = sum(second(18 + k, one, k) for k in range(3))
        g_shift = sum(centre[14 + k] * grad[18 + one][k] for k in range(3))
        gauge = (
            -2.0 * a_lapse
            - lapse * ((4.0 / 3.0) * g_trace + 3.0 * (a_chi * over_chi))
            + lap[18 + one]
            + b_mixed * (1.0 / 3.0)
            + centre[14 + one] * third_div
            - g_shift
        )
        gauges.append(gauge)
        emit(14 + one, advected[14 + one] + gauge)
    emit(17, advected[17] - 2.0 * lapse * (trace - 2.0 * theta))
    for one in range(3):
        emit(18 + one, advected[18 + one] + 0.75 * centre[21 + one])
    for one in range(3):
        emit(21 + one, advected[21 + one] + gauges[one] - DRIVER_ETA * centre[21 + one])
    emit(
        24,
        advected[24]
        + 0.5 * lapse * (chi * ricci_trace + (2.0 / 3.0) * trace * trace - squares)
        - 2.0 * KAPPA_ONE * lapse * theta,
    )


def section_kernel(
    sizes, groups, section, base, accum, ns_out, na_out, slab_out,
    xb, tb, tile, slab, bb, ab, local_sem, halo_send, halo_recv,
    line_send, gather_recv, out_sem,
):
    gx, gy, gz = sizes
    fields, planes, rows, lanes = section.shape
    i, j, k = (lax.axis_index(name) for name in ("gx", "gy", "gz"))
    group = fields // groups

    def device(dx=0, dy=0, dz=0):
        return (
            lax.rem(i + dx + gx, gx),
            lax.rem(j + dy + gy, gy),
            lax.rem(k + dz + gz, gz),
        )

    x_steps = (1,) if gx == 2 else (1, -1)
    messages = []

    def plane_pair(dz):
        if dz == 0:
            return slice(0, planes), slice(2, 2 + planes)
        if dz == 1:
            return slice(planes - 2, planes), slice(0, 2)
        return slice(0, 2), slice(2 + planes, 4 + planes)

    def row_pair(dy):
        if dy == 0:
            return slice(0, rows), slice(PAD, PAD + rows)
        if dy == 1:
            return slice(rows - PAD, rows), slice(0, PAD)
        return slice(0, PAD), slice(PAD + rows, 2 * PAD + rows)

    def at(ref, lead, plane_cut, row_cut):
        def ds(cut):
            return pl.ds(cut.start, cut.stop - cut.start)

        return ref.at[lead, ds(plane_cut), ds(row_cut), :]

    for dz in (1, -1):
        src_p, dst_p = plane_pair(dz)
        src_r, dst_r = row_pair(0)
        whole = pl.ds(0, fields)
        messages.append(((0, 0, dz), at(section, whole, src_p, src_r), at(xb, whole, dst_p, dst_r)))
    for dy in (1, -1):
        src_p, dst_p = plane_pair(0)
        src_r, dst_r = row_pair(dy)
        messages.append(((0, dy, 0), at(section, whole, src_p, src_r), at(xb, whole, dst_p, dst_r)))
    for dy in (1, -1):
        for dz in (1, -1):
            src_p, dst_p = plane_pair(dz)
            src_r, dst_r = row_pair(dy)
            for start, size in MIXED_RUNS:
                run = pl.ds(start, size)
                messages.append(((0, dy, dz), at(section, run, src_p, src_r), at(xb, run, dst_p, dst_r)))
    direct = len(messages)
    for slot, dx in enumerate(x_steps):
        for dy, dz in ((0, 0), (1, 0), (-1, 0), (0, 1), (0, -1)):
            src_p, dst_p = plane_pair(dz)
            src_r, dst_r = row_pair(dy)
            messages.append(((dx, dy, dz), at(tile, 0, src_p, src_r), at(tb, slot, dst_p, dst_r)))

    load_section = pltpu.make_async_copy(
        section,
        xb.at[:, pl.ds(2, planes), pl.ds(PAD, rows), :],
        local_sem.at[0],
    )
    load_base = pltpu.make_async_copy(base, bb, local_sem.at[1])
    load_accum = pltpu.make_async_copy(accum, ab, local_sem.at[2])
    load_section.start()

    partners = []
    for delta, _, _ in messages:
        if delta not in partners:
            partners.append(delta)
    barrier = pltpu.get_barrier_semaphore()
    for delta in partners:
        pl.semaphore_signal(barrier, inc=1, device_id=device(*delta), device_id_type=MESH)
    pl.semaphore_wait(barrier, len(partners))

    copies = [
        pltpu.make_async_remote_copy(
            src_ref=src, dst_ref=dst, send_sem=halo_send.at[m], recv_sem=halo_recv.at[m],
            device_id=device(*delta), device_id_type=MESH,
        )
        for m, (delta, src, dst) in enumerate(messages)
    ]
    load_section.wait()
    lane = lax.broadcasted_iota(jnp.int32, (rows, lanes), 1)

    def pack(plane, carry):
        packed = jnp.zeros((rows, lanes), jnp.float32)
        for field in range(fields):
            value = xb[field, plane + 2, PAD : PAD + rows, :]
            ends = jnp.where(lane < 2, value, pltpu.roll(value, 4, 1))
            if field:
                ends = pltpu.roll(ends, 4 * field, 1)
            packed = jnp.where((lane >> 2) == field, ends, packed)
        tile[0, plane] = packed
        return carry

    lax.fori_loop(0, planes, pack, 0)
    for copy in copies[:direct]:
        copy.start()
    for copy in copies[direct:]:
        copy.start()
    load_base.start()
    load_accum.start()
    load_base.wait()
    load_accum.wait()
    for copy in copies:
        copy.wait_recv()

    own_rows = pl.ds(pl.multiple_of(j * rows, rows), rows)
    own_cols = pl.ds(pl.multiple_of(i * lanes, lanes), lanes)

    def step(plane, carry):
        def emit(field, rate):
            slab[field, plane, own_rows, own_cols] = bb[field, plane] + (0.5 * STEP_DT) * rate
            ab[field, plane] = ab[field, plane] + (STEP_DT / 3.0) * rate

        rates_of_plane(plane, rows, lanes, xb, tb, emit)
        return carry

    lax.fori_loop(0, planes, step, 0)

    def piece(ref, bi, bj, c=None):
        lead = pl.ds(0, fields) if c is None else pl.ds(c * group, group)
        return ref.at[
            lead,
            :,
            pl.ds(pl.multiple_of(bj * rows, rows), rows),
            pl.ds(pl.multiple_of(bi * lanes, lanes), lanes),
        ]

    towards = ((0, 1), (0, -1), (1, 0), (-1, 0))

    def send(link, bi, bj, c):
        dx, dy = towards[link]
        return pltpu.make_async_remote_copy(
            src_ref=piece(slab, bi, bj, c),
            dst_ref=piece(slab, bi, bj, c),
            send_sem=line_send.at[link, bi, bj, c],
            recv_sem=gather_recv.at[bi, bj, c],
            device_id=device(dx, dy, 0),
            device_id_type=MESH,
        )

    def arrive(bi, bj, c):
        part = piece(slab, bi, bj, c)
        pltpu.make_async_remote_copy(
            src_ref=part, dst_ref=part, send_sem=line_send.at[0, bi, bj, c],
            recv_sem=gather_recv.at[bi, bj, c], device_id=device(0, 1, 0),
            device_id_type=MESH,
        ).wait_recv()

    def to_hbm(bi, bj):
        return pltpu.make_async_copy(
            piece(slab, bi, bj), piece(slab_out, bi, bj), out_sem.at[bi, bj]
        )

    paired = gx == 2 and gy % 2 == 0
    turned = (groups * 2) // 5 if paired else 0
    pair = j + 1 - 2 * lax.rem(j, 2)

    def each(count, body, start=0):
        lax.fori_loop(start, count, lambda c, carry: (body(c), carry)[1], 0)

    def x_links(body):
        @pl.when(i + 1 < gx)
        def _():
            body(2)

        @pl.when(i > 0)
        def _():
            body(3)

    def own(c):
        @pl.when(j + 1 < gy)
        def _():
            send(0, i, j, c).start()

        @pl.when(j > 0)
        def _():
            send(1, i, j, c).start()

        x_links(lambda link: send(link, i, j, c).start())

    each(groups, own)
    to_hbm(i, j).start()
    ns_copy = pltpu.make_async_copy(piece(slab, i, j), ns_out, local_sem.at[0])
    na_copy = pltpu.make_async_copy(ab, na_out, local_sem.at[1])
    ns_copy.start()
    na_copy.start()

    def crossed(d, bj, c, body):
        if d == 1 and turned:
            @pl.when((bj != pair) | (c >= turned))
            def _():
                body()
        else:
            body()

    other = 1 - i

    for d in range(1, gy):
        def column(c, d=d):
            @pl.when(j - d >= 0)
            def _():
                bj = j - d
                arrive(i, bj, c)

                @pl.when(j + 1 < gy)
                def _():
                    send(0, i, bj, c).start()

                crossed(d, bj, c, lambda: x_links(lambda link: send(link, i, bj, c).start()))

            @pl.when(j + d < gy)
            def _():
                bj = j + d
                arrive(i, bj, c)

                @pl.when(j > 0)
                def _():
                    send(1, i, bj, c).start()

                crossed(d, bj, c, lambda: x_links(lambda link: send(link, i, bj, c).start()))

            if d == 1 and turned:
                @pl.when(c < turned)
                def _():
                    arrive(other, j, c)

                    @pl.when(pair > j)
                    def _():
                        send(0, other, j, c).start()

                    @pl.when(pair < j)
                    def _():
                        send(1, other, j, c).start()

        each(groups, column)

        @pl.when(j - d >= 0)
        def _():
            to_hbm(i, j - d).start()

        @pl.when(j + d < gy)
        def _():
            to_hbm(i, j + d).start()

    def block_rows(body):
        body(j, True)
        for d in range(1, gy):
            @pl.when(j - d >= 0)
            def _():
                body(j - d, False)

            @pl.when(j + d < gy)
            def _():
                body(j + d, False)

    for d in range(1, gx):
        def row(bj, first, d=d):
            @pl.when(i - d >= 0)
            def _():
                def take(c):
                    arrive(i - d, bj, c)

                    @pl.when(i + 1 < gx)
                    def _():
                        send(2, i - d, bj, c).start()

                each(groups, take, turned if first else 0)
                to_hbm(i - d, bj).start()

            @pl.when(i + d < gx)
            def _():
                def take(c):
                    arrive(i + d, bj, c)

                    @pl.when(i > 0)
                    def _():
                        send(3, i + d, bj, c).start()

                each(groups, take, turned if first else 0)
                to_hbm(i + d, bj).start()

        block_rows(row)

    for copy in copies:
        copy.wait_send()

    def drain(bj):
        def chunk(c):
            @pl.when((bj <= j) & (j + 1 < gy))
            def _():
                send(0, i, bj, c).wait_send()

            @pl.when((bj >= j) & (j > 0))
            def _():
                send(1, i, bj, c).wait_send()

            def sideways(link):
                send(link, i, bj, c).wait_send()

            if turned:
                @pl.when((bj != pair) | (c >= turned))
                def _():
                    x_links(sideways)
            else:
                x_links(sideways)

            for d in range(1, gx):
                @pl.when((i - d >= 0) & (i + 1 < gx))
                def _():
                    send(2, i - d, bj, c).wait_send()

                @pl.when((i + d < gx) & (i > 0))
                def _():
                    send(3, i + d, bj, c).wait_send()

        each(groups, chunk)

    each(gy, drain)
    if turned:
        def drain_turned(c):
            @pl.when(pair > j)
            def _():
                send(0, other, j, c).wait_send()

            @pl.when(pair < j)
            def _():
                send(1, other, j, c).wait_send()

        each(turned, drain_turned)
    for bi in range(gx):
        each(gy, lambda bj, bi=bi: to_hbm(bi, bj).wait())
    ns_copy.wait()
    na_copy.wait()


def shards(sizes, section, base, accum):
    gx, gy, gz = sizes
    fields, planes, rows, lanes = section.shape
    groups = 5
    slots = 1 if gx == 2 else 2
    n_messages = 4 + 4 * len(MIXED_RUNS) + 5 * slots
    any_spec = pl.BlockSpec(memory_space=pl.ANY)
    block = jax.ShapeDtypeStruct(section.shape, jnp.float32)
    slab = jax.ShapeDtypeStruct((fields, planes, gy * rows, gx * lanes), jnp.float32)
    dma = pltpu.SemaphoreType.DMA
    return pl.pallas_call(
        functools.partial(section_kernel, sizes, groups),
        out_shape=(block, block, slab),
        in_specs=[any_spec] * 3,
        out_specs=(any_spec,) * 3,
        scratch_shapes=[
            pltpu.VMEM((fields, planes + 4, rows + 2 * PAD, lanes), jnp.float32),
            pltpu.VMEM((slots, planes + 4, rows + 2 * PAD, lanes), jnp.float32),
            pltpu.VMEM((1, planes, rows, lanes), jnp.float32),
            pltpu.VMEM(slab.shape, jnp.float32),
            pltpu.VMEM(section.shape, jnp.float32),
            pltpu.VMEM(section.shape, jnp.float32),
            dma((3,)),
            dma((n_messages,)),
            dma((n_messages,)),
            dma((4, gx, gy, groups)),
            dma((gx, gy, groups)),
            dma((gx, gy)),
        ],
        compiler_params=pltpu.CompilerParams(collective_id=0, has_side_effects=True),
    )(section, base, accum)


def solution(mesh):
    sizes = tuple(mesh.shape[name] for name in ("gx", "gy", "gz"))
    spec = P(None, "gz", "gy", "gx")
    return jax.shard_map(
        functools.partial(shards, sizes),
        mesh=mesh,
        in_specs=(spec, spec, spec),
        out_specs=(spec, spec, P(None, "gz", None, None)),
        check_vma=False,
    )
```

time: 148 us -> 69.3 us (0.47)
  waiting for transfers between devices: 107 us -> 0 us
  Pallas kernels: 0 us -> 60.8 us
  between operations: 14.3 us -> 0.64 us
  other arithmetic: 7.84 us -> 0 us
  starting transfers between devices: 7.67 us -> 0 us
  local copies, waits for them, and re-layouts: 11.2 us -> 7.56 us
    all_gather x1 -> x0, waiting for transfers between devices: 61.4 us -> none  [shards(): lax.all_gather(next_section[None], ('gx', 'gy'), axis=0, tiled=True)]
    pallas_call x0 -> x1, Pallas kernels: none -> 60.8 us  [shards(): pl.pallas_call(functools.partial(section_kernel, sizes, groups), out_shap...]
    ppermute x6 -> x0, waiting for transfers between devices: 45.2 us -> none  [the longest x3 28.5 us: extended(): lax.ppermute(lax.slice_in_dim(block, 0, width, axis=dim), axis, backward)]
    ppermute x6 -> x0, starting transfers between devices: 7.63 us -> none  [the longest x3 5.41 us: extended(): lax.ppermute(lax.slice_in_dim(block, block.shape[dim] - width, None, axis...]
    unnamed x6 -> x3, local copies, waits for them, and re-layouts: 0.72 us -> 7.56 us
    add x9 -> x0, other arithmetic: 5.89 us -> none  [the longest x4 2.43 us: line_sum(): running = weighted if running is None else running + weighted]
    transpose x1 -> x0, local copies, waits for them, and re-layouts: 4.46 us -> none  [shards(): regrouped = jnp.transpose(regrouped, (2, 3, 1, 4, 0, 5))]
    reshape x1 -> x0, local copies, waits for them, and re-layouts: 3.82 us -> none  [shards(): regrouped.reshape(fields_count, planes, height_parts * block_rows, width_...]
  transfers between devices with their start and end apart: 7 -> 0, of which waited for: 7 -> 0; matrix products, arithmetic and copies ran while one was open for 1% -> 0% of each run, Pallas kernels for 0% -> 0%
where the time goes in v1:
time: 69.3 us; the launch traced here: 69 us
  Pallas kernels  60.8 us (88%)
  local copies, waits for them, and re-layouts  7.56 us (11%)
    pallas_call x1, Pallas kernels, shards(): pl.pallas_call(functools.partial(section_kernel, sizes, groups), out_shap...  60.8 us
    unnamed x3, local copies, waits for them, and re-layouts  7.56 us

profile of v1, /device:TPU:0, one launch (start us, length us, event | category | flops | bytes accessed | tf_op | source)
XLA Modules:
  0.0 69.0 jit_solution(6507513377944382916)
XLA Ops:
  0.6 60.8 %shard_map.58 = (f32[25,2,16,128]{3,2,1,0:T(8,128)}, f32[25,2,16,128]{3,2,1,0:T(8,128)}, f32[25,2,64,256]{3,2,1,0:T(8,128)}) custom-call(f32[25,2,16,128]{3,2,1,0:T(8,128)} %section.1, f32[25,2,16,128]{3,2,1,0:T(8,128)} %base.1, f32[25,2,16,128]{3,2,1,0:T(8,128)} %accum.1), custom_call_target="tpu_custom_call" | custom-call | tf_op jit(solution)/shard_map/pallas_call | solution.py:580
  61.4 1.8 %copy.9 = f32[25,2,16,128]{3,2,1,0:T(8,128)} copy(f32[25,2,16,128]{3,2,1,0:T(8,128)} %get-tuple-element.6) | data formatting | bytes 819200
  63.2 1.8 %copy.10 = f32[25,2,16,128]{3,2,1,0:T(8,128)} copy(f32[25,2,16,128]{3,2,1,0:T(8,128)} %get-tuple-element.7) | data formatting | bytes 819200
  65.0 4.0 %copy.11 = f32[25,2,64,256]{3,2,1,0:T(8,128)} copy(f32[25,2,64,256]{3,2,1,0:T(8,128)} %get-tuple-element.8) | data formatting | bytes 6553600

commit v2 on v1

--- a/solution.py
+++ b/solution.py
@@ -224,9 +224,9 @@
 
 
 def section_kernel(
-    sizes, groups, section, base, accum, ns_out, na_out, slab_out,
-    xb, tb, tile, slab, bb, ab, local_sem, halo_send, halo_recv,
-    line_send, gather_recv, out_sem,
+    sizes, groups, section, base, accum, ns_out, na_out, slab,
+    xb, tb, tile, bb, ab, local_sem, halo_send, halo_recv,
+    line_send, gather_recv,
 ):
     gx, gy, gz = sizes
     fields, planes, rows, lanes = section.shape
@@ -254,8 +254,8 @@
         if dy == 0:
             return slice(0, rows), slice(PAD, PAD + rows)
         if dy == 1:
-            return slice(rows - PAD, rows), slice(0, PAD)
-        return slice(0, PAD), slice(PAD + rows, 2 * PAD + rows)
+            return slice(rows - 2, rows), slice(PAD - 2, PAD)
+        return slice(0, 2), slice(PAD + rows, PAD + rows + 2)
 
     def at(ref, lead, plane_cut, row_cut):
         def ds(cut):
@@ -343,7 +343,8 @@
     def step(plane, carry):
         def emit(field, rate):
             slab[field, plane, own_rows, own_cols] = bb[field, plane] + (0.5 * STEP_DT) * rate
-            ab[field, plane] = ab[field, plane] + (STEP_DT / 3.0) * rate
+            ns_out[field, plane] = bb[field, plane] + (0.5 * STEP_DT) * rate
+            na_out[field, plane] = ab[field, plane] + (STEP_DT / 3.0) * rate
 
         rates_of_plane(plane, rows, lanes, xb, tb, emit)
         return carry
@@ -380,11 +381,6 @@
             device_id_type=MESH,
         ).wait_recv()
 
-    def to_hbm(bi, bj):
-        return pltpu.make_async_copy(
-            piece(slab, bi, bj), piece(slab_out, bi, bj), out_sem.at[bi, bj]
-        )
-
     paired = gx == 2 and gy % 2 == 0
     turned = (groups * 2) // 5 if paired else 0
     pair = j + 1 - 2 * lax.rem(j, 2)
@@ -413,11 +409,6 @@
         x_links(lambda link: send(link, i, j, c).start())
 
     each(groups, own)
-    to_hbm(i, j).start()
-    ns_copy = pltpu.make_async_copy(piece(slab, i, j), ns_out, local_sem.at[0])
-    na_copy = pltpu.make_async_copy(ab, na_out, local_sem.at[1])
-    ns_copy.start()
-    na_copy.start()
 
     def crossed(d, bj, c, body):
         if d == 1 and turned:
@@ -470,11 +461,11 @@
 
         @pl.when(j - d >= 0)
         def _():
-            to_hbm(i, j - d).start()
+            pass
 
         @pl.when(j + d < gy)
         def _():
-            to_hbm(i, j + d).start()
+            pass
 
     def block_rows(body):
         body(j, True)
@@ -499,7 +490,7 @@
                         send(2, i - d, bj, c).start()
 
                 each(groups, take, turned if first else 0)
-                to_hbm(i - d, bj).start()
+                pass
 
             @pl.when(i + d < gx)
             def _():
@@ -511,7 +502,7 @@
                         send(3, i + d, bj, c).start()
 
                 each(groups, take, turned if first else 0)
-                to_hbm(i + d, bj).start()
+                pass
 
         block_rows(row)
 
@@ -561,10 +552,15 @@
                 send(1, other, j, c).wait_send()
 
         each(turned, drain_turned)
-    for bi in range(gx):
-        each(gy, lambda bj, bi=bi: to_hbm(bi, bj).wait())
-    ns_copy.wait()
-    na_copy.wait()
+
+
+def put_out(ns_in, na_in, slab_in, ns_out, na_out, slab_out, sem):
+    pairs = ((slab_in, slab_out), (ns_in, ns_out), (na_in, na_out))
+    copies = [pltpu.make_async_copy(a, b, sem.at[n]) for n, (a, b) in enumerate(pairs)]
+    for copy in copies:
+        copy.start()
+    for copy in copies:
+        copy.wait()
 
 
 def shards(sizes, section, base, accum):
@@ -577,16 +573,15 @@
     block = jax.ShapeDtypeStruct(section.shape, jnp.float32)
     slab = jax.ShapeDtypeStruct((fields, planes, gy * rows, gx * lanes), jnp.float32)
     dma = pltpu.SemaphoreType.DMA
-    return pl.pallas_call(
+    staged = pl.pallas_call(
         functools.partial(section_kernel, sizes, groups),
         out_shape=(block, block, slab),
-        in_specs=[any_spec] * 3,
-        out_specs=(any_spec,) * 3,
+        in_specs=[pl.BlockSpec(memory_space=pltpu.HBM)] * 3,
+        out_specs=(pl.BlockSpec(memory_space=pltpu.VMEM),) * 3,
         scratch_shapes=[
             pltpu.VMEM((fields, planes + 4, rows + 2 * PAD, lanes), jnp.float32),
             pltpu.VMEM((slots, planes + 4, rows + 2 * PAD, lanes), jnp.float32),
             pltpu.VMEM((1, planes, rows, lanes), jnp.float32),
-            pltpu.VMEM(slab.shape, jnp.float32),
             pltpu.VMEM(section.shape, jnp.float32),
             pltpu.VMEM(section.shape, jnp.float32),
             dma((3,)),
@@ -594,10 +589,17 @@
             dma((n_messages,)),
             dma((4, gx, gy, groups)),
             dma((gx, gy, groups)),
-            dma((gx, gy)),
         ],
-        compiler_params=pltpu.CompilerParams(collective_id=0, has_side_effects=True),
+        compiler_params=pltpu.CompilerParams(collective_id=0, has_side_effects=True, vmem_limit_bytes=24 << 20),
     )(section, base, accum)
+    return pl.pallas_call(
+        put_out,
+        out_shape=(block, block, slab),
+        in_specs=[pl.BlockSpec(memory_space=pltpu.VMEM)] * 3,
+        out_specs=(any_spec,) * 3,
+        scratch_shapes=[dma((3,))],
+        compiler_params=pltpu.CompilerParams(vmem_limit_bytes=8 << 20),
+    )(*staged)
 
 
 def solution(mesh):

time: 69.3 us -> 62.1 us (0.90)
  local copies, waits for them, and re-layouts: 7.56 us -> 3 us
  Pallas kernels: 60.8 us -> 58.2 us
    pallas_call x1, Pallas kernels: 60.8 us -> 56.2 us  [shards(): pl.pallas_call(functools.partial(section_kernel, sizes, groups), out_shap...]
    unnamed x3 -> x6, local copies, waits for them, and re-layouts: 7.56 us -> 3 us
    pallas_call x0 -> x1, Pallas kernels: none -> 1.99 us  [shards(): pl.pallas_call(put_out, out_shape=(block, block, slab), in_specs=[pl.Bloc...]
where the time goes in v2:
time: 62.1 us; the launch traced here: 61.9 us
  Pallas kernels  58.2 us (94%)
  local copies, waits for them, and re-layouts  3 us (5%)
  between operations  0.65 us (1%)
    pallas_call x1, Pallas kernels, shards(): pl.pallas_call(functools.partial(section_kernel, sizes, groups), out_shap...  56.2 us
    unnamed x6, local copies, waits for them, and re-layouts  3 us
    pallas_call x1, Pallas kernels, shards(): pl.pallas_call(put_out, out_shape=(block, block, slab), in_specs=[pl.Bloc...  1.99 us

profile of v2, /device:TPU:0, one launch (start us, length us, event | category | flops | bytes accessed | tf_op | source)
XLA Modules:
  0.0 61.9 jit_solution(10694976389828075002)
XLA Ops:
  0.6 0.0 copy-start
  0.6 1.0 %copy-done = f32[25,2,16,128]{3,2,1,0:T(8,128)S(1)} copy-done((f32[25,2,16,128]{3,2,1,0:T(8,128)S(1)}, f32[25,2,16,128]{3,2,1,0:T(8,128)}, u32[]{:S(2)}) %copy-start) | copy-done | bytes 409624
  1.6 0.0 copy-start.1
  1.6 1.0 %copy-done.1 = f32[25,2,16,128]{3,2,1,0:T(8,128)S(1)} copy-done((f32[25,2,16,128]{3,2,1,0:T(8,128)S(1)}, f32[25,2,16,128]{3,2,1,0:T(8,128)}, u32[]{:S(2)}) %copy-start.1) | copy-done | bytes 409624
  2.6 0.0 copy-start.2
  2.6 1.0 %copy-done.2 = f32[25,2,16,128]{3,2,1,0:T(8,128)S(1)} copy-done((f32[25,2,16,128]{3,2,1,0:T(8,128)S(1)}, f32[25,2,16,128]{3,2,1,0:T(8,128)}, u32[]{:S(2)}) %copy-start.2) | copy-done | bytes 409624
  3.6 56.2 %shard_map.58 = (f32[25,2,16,128]{3,2,1,0:T(8,128)S(1)}, f32[25,2,16,128]{3,2,1,0:T(8,128)S(1)}, f32[25,2,64,256]{3,2,1,0:T(8,128)S(1)}) custom-call(f32[25,2,16,128]{3,2,1,0:T(8,128)S(1)} %copy-done, f32[25,2,16,128]{3,2,1,0:T(8,128)S(1)} %copy-done.1, f32[25,2,16,128]{3,2,1,0:T(8,128)S(1)} %copy-done.2), custom_call_target="tpu_custom_call" | custom-call | tf_op jit(solution)/shard_map/pallas_call | solution.py:576
  59.9 2.0 %shard_map.59 = (f32[25,2,16,128]{3,2,1,0:T(8,128)}, f32[25,2,16,128]{3,2,1,0:T(8,128)}, f32[25,2,64,256]{3,2,1,0:T(8,128)}) custom-call(f32[25,2,16,128]{3,2,1,0:T(8,128)S(1)} %get-tuple-element.6.ns_in, f32[25,2,16,128]{3,2,1,0:T(8,128)S(1)} %get-tuple-element.7.na_in, f32[25,2,64,256]{3,2,1,0:T(8,128)S(1)} %get-tuple-element.8.slab_in), custom_call_target="tpu_custom_call" | custom-call | tf_op jit(solution)/shard_map/pallas_call | solution.py:595
Async XLA Ops:
  0.6 1.0 %copy-start = (f32[25,2,16,128]{3,2,1,0:T(8,128)S(1)}, f32[25,2,16,128]{3,2,1,0:T(8,128)}, u32[]{:S(2)}) copy-start(f32[25,2,16,128]{3,2,1,0:T(8,128)} %section.1) | copy-start | bytes 1228804
  1.6 1.0 %copy-start.1 = (f32[25,2,16,128]{3,2,1,0:T(8,128)S(1)}, f32[25,2,16,128]{3,2,1,0:T(8,128)}, u32[]{:S(2)}) copy-start(f32[25,2,16,128]{3,2,1,0:T(8,128)} %base.1) | copy-start | bytes 1228804
  2.6 1.0 %copy-start.2 = (f32[25,2,16,128]{3,2,1,0:T(8,128)S(1)}, f32[25,2,16,128]{3,2,1,0:T(8,128)}, u32[]{:S(2)}) copy-start(f32[25,2,16,128]{3,2,1,0:T(8,128)} %accum.1) | copy-start | bytes 1228804

commit v3 on v2

--- a/solution.py
+++ b/solution.py
@@ -15,7 +15,10 @@
 PAIR_LIST = ((0, 0), (0, 1), (0, 2), (1, 1), (1, 2), (2, 2))
 MESH = pl.DeviceIdType.MESH
 MIXED = (0, 17, 18, 19, 20)
-MIXED_RUNS = ((0, 1), (17, 4))
+RUNS = ((0, 1), (17, 4), (1, 5), (6, 2), (14, 3), (8, 5), (13, 1), (21, 4))
+GROUPS = 5
+ORDER = tuple(first + n for first, size in RUNS for n in range(size))
+PLACE = tuple(ORDER.index(field) for field in range(len(ORDER)))
 PAD = 8
 
 
@@ -30,7 +33,7 @@
     edge_two = (lane < 2) | (lane >= lanes - 2)
 
     def cell(field, dz=0, dy=0):
-        return xb[field, plane + 2 + dz, PAD + dy : PAD + dy + rows, :]
+        return xb[PLACE[field], plane + 2 + dz, PAD + dy : PAD + dy + rows, :]
 
     def strip(dz=0, dy=0):
         def side(slot):
@@ -68,12 +71,15 @@
     edge_z = first_of(*z_line(strip))
     edge_z_in = inner(edge_z)
 
-    centre, grad, curve, lap, smooth, mixed = {}, {}, {}, {}, {}, {}
+    centre, grad, curve, lap, mixed = {}, {}, {}, {}, {}
     need_lap = (0, 1, 2, 3, 4, 5, 6, 17, 18, 19, 20)
     shift = [cell(18), cell(19), cell(20)]
     advected = {}
-    for field in range(25):
-        value = cell(field)
+    for field in range(len(ORDER)):
+        centre[field] = cell(field)
+
+    def differentiate(field):
+        value = centre[field]
         read = functools.partial(cell, field)
         lines = [x_line(field, value, edge, edge_in), y_line(read), z_line(read)]
         near = [m1 + p1 for _, m1, p1, _ in lines]
@@ -82,7 +88,6 @@
         far_sum = far[0] + far[1] + far[2]
         smooth = far_sum - 4.0 * near_sum + 18.0 * value
         grads = [first_of(*line) for line in lines]
-        centre[field] = value
         grad[field] = grads
         advected[field] = (
             shift[0] * grads[0] + shift[1] * grads[1] + shift[2] * grads[2]
@@ -122,34 +127,11 @@
         (2.0 - metric[k]) if one == two else -metric[k]
         for k, (one, two) in enumerate(PAIR_LIST)
     ]
-    count = [1.0 if one == two else 2.0 for one, two in PAIR_LIST]
 
     def contract(left, right):
         diag = left[0] * right[0] + left[3] * right[3] + left[5] * right[5]
         off = left[1] * right[1] + left[2] * right[2] + left[4] * right[4]
         return diag + 2.0 * off
-
-    chi, trace, lapse, theta = centre[0], centre[7], centre[17], centre[24]
-    div = grad[18][0] + grad[19][1] + grad[20][2]
-    third_div = (2.0 / 3.0) * div
-    squares = contract(traceless, traceless)
-    over_chi = 1.0 / chi
-    half_over = 0.5 * over_chi
-    lapse_dd = [second(17, one, two) for one, two in PAIR_LIST]
-    ricci = []
-    for k, (one, two) in enumerate(PAIR_LIST):
-        conf = second(0, one, two)
-        if one == two:
-            conf = conf + lap[0]
-            grads_g = grad[14 + one][one]
-        else:
-            grads_g = 0.5 * (grad[14 + two][one] + grad[14 + one][two])
-        ricci.append(-0.5 * lap[1 + k] + grads_g + conf * half_over)
-    ricci_trace = contract(inverse, ricci)
-    lapse_trace = contract(inverse, lapse_dd)
-    source_trace = lapse * ricci_trace - lapse_trace
-
-    emit(0, advected[0] + (2.0 / 3.0) * chi * (lapse * trace) - chi * third_div)
 
     def lie_of(table, one, two):
         total = None
@@ -164,7 +146,25 @@
             total = term if total is None else total + term
         return total
 
-    for k, (one, two) in enumerate(PAIR_LIST):
+    group = len(ORDER) // GROUPS
+
+    def begin(stage):
+        for field in ORDER[stage * group : (stage + 1) * group]:
+            differentiate(field)
+
+    chi, trace, lapse, theta = centre[0], centre[7], centre[17], centre[24]
+
+    begin(0)
+    div = grad[18][0] + grad[19][1] + grad[20][2]
+    third_div = (2.0 / 3.0) * div
+    emit(0, advected[0] + (2.0 / 3.0) * chi * (lapse * trace) - chi * third_div)
+    emit(17, advected[17] - 2.0 * lapse * (trace - 2.0 * theta))
+    for one in range(3):
+        emit(18 + one, advected[18 + one] + 0.75 * centre[21 + one])
+    yield
+
+    def metric_rate(k):
+        one, two = PAIR_LIST[k]
         emit(
             1 + k,
             advected[1 + k]
@@ -172,6 +172,19 @@
             + lie_of(metric, one, two)
             - metric[k] * third_div,
         )
+
+    begin(1)
+    for k in range(5):
+        metric_rate(k)
+    yield
+
+    begin(2)
+    metric_rate(5)
+    over_chi = 1.0 / chi
+    half_over = 0.5 * over_chi
+    squares = contract(traceless, traceless)
+    lapse_dd = [second(17, one, two) for one, two in PAIR_LIST]
+    lapse_trace = contract(inverse, lapse_dd)
     emit(
         7,
         advected[7]
@@ -179,20 +192,6 @@
         + lapse * (squares + trace * trace * (1.0 / 3.0))
         + KAPPA_ONE * lapse * theta,
     )
-    third_trace = source_trace * (1.0 / 3.0)
-    for k, (one, two) in enumerate(PAIR_LIST):
-        free = lapse * ricci[k] - lapse_dd[k] - metric[k] * third_trace
-        product = sum(
-            sym(traceless, one, m) * sym(traceless, m, two) for m in range(3)
-        )
-        emit(
-            8 + k,
-            advected[8 + k]
-            + chi * free
-            + lapse * (trace * traceless[k] - 2.0 * product)
-            + lie_of(traceless, one, two)
-            - traceless[k] * third_div,
-        )
     gauges = []
     for one in range(3):
         a_lapse = sum(sym(traceless, one, k) * grad[17][k] for k in range(3))
@@ -210,9 +209,42 @@
         )
         gauges.append(gauge)
         emit(14 + one, advected[14 + one] + gauge)
-    emit(17, advected[17] - 2.0 * lapse * (trace - 2.0 * theta))
-    for one in range(3):
-        emit(18 + one, advected[18 + one] + 0.75 * centre[21 + one])
+    yield
+
+    begin(3)
+    ricci = []
+    for k, (one, two) in enumerate(PAIR_LIST):
+        conf = second(0, one, two)
+        if one == two:
+            conf = conf + lap[0]
+            grads_g = grad[14 + one][one]
+        else:
+            grads_g = 0.5 * (grad[14 + two][one] + grad[14 + one][two])
+        ricci.append(-0.5 * lap[1 + k] + grads_g + conf * half_over)
+    ricci_trace = contract(inverse, ricci)
+    third_trace = (lapse * ricci_trace - lapse_trace) * (1.0 / 3.0)
+
+    def traceless_rate(k):
+        one, two = PAIR_LIST[k]
+        free = lapse * ricci[k] - lapse_dd[k] - metric[k] * third_trace
+        product = sum(
+            sym(traceless, one, m) * sym(traceless, m, two) for m in range(3)
+        )
+        emit(
+            8 + k,
+            advected[8 + k]
+            + chi * free
+            + lapse * (trace * traceless[k] - 2.0 * product)
+            + lie_of(traceless, one, two)
+            - traceless[k] * third_div,
+        )
+
+    for k in range(5):
+        traceless_rate(k)
+    yield
+
+    begin(4)
+    traceless_rate(5)
     for one in range(3):
         emit(21 + one, advected[21 + one] + gauges[one] - DRIVER_ETA * centre[21 + one])
     emit(
@@ -221,6 +253,7 @@
         + 0.5 * lapse * (chi * ricci_trace + (2.0 / 3.0) * trace * trace - squares)
         - 2.0 * KAPPA_ONE * lapse * theta,
     )
+    yield
 
 
 def section_kernel(
@@ -263,37 +296,56 @@
 
         return ref.at[lead, ds(plane_cut), ds(row_cut), :]
 
-    for dz in (1, -1):
-        src_p, dst_p = plane_pair(dz)
-        src_r, dst_r = row_pair(0)
-        whole = pl.ds(0, fields)
-        messages.append(((0, 0, dz), at(section, whole, src_p, src_r), at(xb, whole, dst_p, dst_r)))
-    for dy in (1, -1):
-        src_p, dst_p = plane_pair(0)
-        src_r, dst_r = row_pair(dy)
-        messages.append(((0, dy, 0), at(section, whole, src_p, src_r), at(xb, whole, dst_p, dst_r)))
-    for dy in (1, -1):
-        for dz in (1, -1):
-            src_p, dst_p = plane_pair(dz)
-            src_r, dst_r = row_pair(dy)
-            for start, size in MIXED_RUNS:
-                run = pl.ds(start, size)
-                messages.append(((0, dy, dz), at(section, run, src_p, src_r), at(xb, run, dst_p, dst_r)))
+    def own(cut_p, cut_r):
+        return (
+            slice(cut_p.start + 2, cut_p.stop + 2),
+            slice(cut_r.start + PAD, cut_r.stop + PAD),
+        )
+
+    stages = [[] for _ in range(groups)]
+
+    def add(stage, delta, src, dst):
+        stages[stage].append(len(messages))
+        messages.append((delta, src, dst))
+
+    def face(stage, delta):
+        src_p, dst_p = plane_pair(delta[2])
+        src_r, dst_r = row_pair(delta[1])
+        run = pl.ds(stage * group, group)
+        add(stage, delta, at(xb, run, *own(src_p, src_r)), at(xb, run, dst_p, dst_r))
+
+    for stage in range(groups):
+        for step in (1, -1):
+            face(stage, (0, step, 0))
+            face(stage, (0, 0, step))
+        if stage == 0:
+            for dy in (1, -1):
+                for dz in (1, -1):
+                    face(0, (0, dy, dz))
     direct = len(messages)
     for slot, dx in enumerate(x_steps):
         for dy, dz in ((0, 0), (1, 0), (-1, 0), (0, 1), (0, -1)):
             src_p, dst_p = plane_pair(dz)
             src_r, dst_r = row_pair(dy)
-            messages.append(((dx, dy, dz), at(tile, 0, src_p, src_r), at(tb, slot, dst_p, dst_r)))
-
-    load_section = pltpu.make_async_copy(
-        section,
-        xb.at[:, pl.ds(2, planes), pl.ds(PAD, rows), :],
-        local_sem.at[0],
-    )
-    load_base = pltpu.make_async_copy(base, bb, local_sem.at[1])
-    load_accum = pltpu.make_async_copy(accum, ab, local_sem.at[2])
-    load_section.start()
+            add(0, (dx, dy, dz), at(tile, 0, src_p, src_r), at(tb, slot, dst_p, dst_r))
+
+    loads = []
+    place = 0
+    for first, size in RUNS:
+        loads.append(
+            pltpu.make_async_copy(
+                section.at[pl.ds(first, size)],
+                xb.at[pl.ds(place, size), pl.ds(2, planes), pl.ds(PAD, rows), :],
+                local_sem.at[2 + len(loads)],
+            )
+        )
+        place += size
+    load_base = pltpu.make_async_copy(base, bb, local_sem.at[0])
+    load_accum = pltpu.make_async_copy(accum, ab, local_sem.at[1])
+    for load in loads:
+        load.start()
+    load_base.start()
+    load_accum.start()
 
     partners = []
     for delta, _, _ in messages:
@@ -311,13 +363,16 @@
         )
         for m, (delta, src, dst) in enumerate(messages)
     ]
-    load_section.wait()
+    for load in loads:
+        load.wait()
+    for copy in copies[:direct]:
+        copy.start()
     lane = lax.broadcasted_iota(jnp.int32, (rows, lanes), 1)
 
     def pack(plane, carry):
         packed = jnp.zeros((rows, lanes), jnp.float32)
         for field in range(fields):
-            value = xb[field, plane + 2, PAD : PAD + rows, :]
+            value = xb[PLACE[field], plane + 2, PAD : PAD + rows, :]
             ends = jnp.where(lane < 2, value, pltpu.roll(value, 4, 1))
             if field:
                 ends = pltpu.roll(ends, 4 * field, 1)
@@ -326,30 +381,13 @@
         return carry
 
     lax.fori_loop(0, planes, pack, 0)
-    for copy in copies[:direct]:
-        copy.start()
     for copy in copies[direct:]:
         copy.start()
-    load_base.start()
-    load_accum.start()
     load_base.wait()
     load_accum.wait()
-    for copy in copies:
-        copy.wait_recv()
 
     own_rows = pl.ds(pl.multiple_of(j * rows, rows), rows)
     own_cols = pl.ds(pl.multiple_of(i * lanes, lanes), lanes)
-
-    def step(plane, carry):
-        def emit(field, rate):
-            slab[field, plane, own_rows, own_cols] = bb[field, plane] + (0.5 * STEP_DT) * rate
-            ns_out[field, plane] = bb[field, plane] + (0.5 * STEP_DT) * rate
-            na_out[field, plane] = ab[field, plane] + (STEP_DT / 3.0) * rate
-
-        rates_of_plane(plane, rows, lanes, xb, tb, emit)
-        return carry
-
-    lax.fori_loop(0, planes, step, 0)
 
     def piece(ref, bi, bj, c=None):
         lead = pl.ds(0, fields) if c is None else pl.ds(c * group, group)
@@ -397,7 +435,7 @@
         def _():
             body(3)
 
-    def own(c):
+    def send_own(c):
         @pl.when(j + 1 < gy)
         def _():
             send(0, i, j, c).start()
@@ -408,7 +446,34 @@
 
         x_links(lambda link: send(link, i, j, c).start())
 
-    each(groups, own)
+    def emit_at(plane):
+        def emit(field, rate):
+            moved = bb[field, plane] + (0.5 * STEP_DT) * rate
+            slab[PLACE[field], plane, own_rows, own_cols] = moved
+            ns_out[field, plane] = moved
+            na_out[field, plane] = ab[field, plane] + (STEP_DT / 3.0) * rate
+
+        return emit
+
+    def await_rows(stage, along_y):
+        for m in stages[stage]:
+            if (messages[m][0][2] == 0) == along_y:
+                copies[m].wait_recv()
+
+    await_rows(0, True)
+    await_rows(0, False)
+    work = [
+        rates_of_plane(plane, rows, lanes, xb, tb, emit_at(plane))
+        for plane in range(planes)
+    ]
+    for stage in range(groups):
+        for part in work:
+            next(part)
+        if stage + 1 < groups:
+            await_rows(stage + 1, True)
+        send_own(stage)
+        if stage + 1 < groups:
+            await_rows(stage + 1, False)
 
     def crossed(d, bj, c, body):
         if d == 1 and turned:
@@ -555,7 +620,12 @@
 
 
 def put_out(ns_in, na_in, slab_in, ns_out, na_out, slab_out, sem):
-    pairs = ((slab_in, slab_out), (ns_in, ns_out), (na_in, na_out))
+    pairs = []
+    place = 0
+    for first, size in RUNS:
+        pairs.append((slab_in.at[pl.ds(place, size)], slab_out.at[pl.ds(first, size)]))
+        place += size
+    pairs += [(ns_in, ns_out), (na_in, na_out)]
     copies = [pltpu.make_async_copy(a, b, sem.at[n]) for n, (a, b) in enumerate(pairs)]
     for copy in copies:
         copy.start()
@@ -566,16 +636,16 @@
 def shards(sizes, section, base, accum):
     gx, gy, gz = sizes
     fields, planes, rows, lanes = section.shape
-    groups = 5
+    groups = GROUPS
     slots = 1 if gx == 2 else 2
-    n_messages = 4 + 4 * len(MIXED_RUNS) + 5 * slots
+    n_messages = 4 * groups + 4 + 5 * slots
     any_spec = pl.BlockSpec(memory_space=pl.ANY)
     block = jax.ShapeDtypeStruct(section.shape, jnp.float32)
     slab = jax.ShapeDtypeStruct((fields, planes, gy * rows, gx * lanes), jnp.float32)
     dma = pltpu.SemaphoreType.DMA
     staged = pl.pallas_call(
         functools.partial(section_kernel, sizes, groups),
-        out_shape=(block, block, slab),
+        out_shape=tuple(pltpu.VMEM(a.shape, a.dtype) for a in (block, block, slab)),
         in_specs=[pl.BlockSpec(memory_space=pltpu.HBM)] * 3,
         out_specs=(pl.BlockSpec(memory_space=pltpu.VMEM),) * 3,
         scratch_shapes=[
@@ -584,20 +654,20 @@
             pltpu.VMEM((1, planes, rows, lanes), jnp.float32),
             pltpu.VMEM(section.shape, jnp.float32),
             pltpu.VMEM(section.shape, jnp.float32),
-            dma((3,)),
+            dma((2 + len(RUNS),)),
             dma((n_messages,)),
             dma((n_messages,)),
             dma((4, gx, gy, groups)),
             dma((gx, gy, groups)),
         ],
         compiler_params=pltpu.CompilerParams(collective_id=0, has_side_effects=True, vmem_limit_bytes=24 << 20),
-    )(section, base, accum)
+    )(*(pltpu.with_memory_space_constraint(x, pltpu.HBM) for x in (section, base, accum)))
     return pl.pallas_call(
         put_out,
         out_shape=(block, block, slab),
         in_specs=[pl.BlockSpec(memory_space=pltpu.VMEM)] * 3,
         out_specs=(any_spec,) * 3,
-        scratch_shapes=[dma((3,))],
+        scratch_shapes=[dma((2 + len(RUNS),))],
         compiler_params=pltpu.CompilerParams(vmem_limit_bytes=8 << 20),
     )(*staged)
 

time: 62.1 us -> 58.2 us (0.937)
  local copies, waits for them, and re-layouts: 3 us -> 0 us
  Pallas kernels: 58.2 us -> 57.5 us
    unnamed x6 -> x0, local copies, waits for them, and re-layouts: 3 us -> none
    pallas_call x1, Pallas kernels: 56.2 us -> 55.4 us  [shards(): pl.pallas_call(functools.partial(section_kernel, sizes, groups), out_shap...]
where the time goes in v3:
time: 58.2 us; the launch traced here: 58.1 us
  Pallas kernels  57.5 us (99%)
  between operations  0.64 us (1%)
    pallas_call x1, Pallas kernels, shards(): pl.pallas_call(functools.partial(section_kernel, sizes, groups), out_shap...  55.4 us
    pallas_call x1, Pallas kernels, shards(): pl.pallas_call(put_out, out_shape=(block, block, slab), in_specs=[pl.Bloc...  2.05 us

profile of v3, /device:TPU:0, one launch (start us, length us, event | category | flops | bytes accessed | tf_op | source)
XLA Modules:
  0.0 58.1 jit_solution(3774830683964383979)
XLA Ops:
  0.6 55.4 %shard_map.58 = (f32[25,2,16,128]{3,2,1,0:T(8,128)S(1)}, f32[25,2,16,128]{3,2,1,0:T(8,128)S(1)}, f32[25,2,64,256]{3,2,1,0:T(8,128)S(1)}) custom-call(f32[25,2,16,128]{3,2,1,0:T(8,128)} %section.1, f32[25,2,16,128]{3,2,1,0:T(8,128)} %base.1, f32[25,2,16,128]{3,2,1,0:T(8,128)} %accum.1), custom_call_target="tpu_custom_call" | custom-call | tf_op jit(solution)/shard_map/pallas_call | solution.py:646
  56.0 2.1 %shard_map.59 = (f32[25,2,16,128]{3,2,1,0:T(8,128)}, f32[25,2,16,128]{3,2,1,0:T(8,128)}, f32[25,2,64,256]{3,2,1,0:T(8,128)}) custom-call(f32[25,2,16,128]{3,2,1,0:T(8,128)S(1)} %get-tuple-element.6.ns_in, f32[25,2,16,128]{3,2,1,0:T(8,128)S(1)} %get-tuple-element.7.na_in, f32[25,2,64,256]{3,2,1,0:T(8,128)S(1)} %get-tuple-element.8.slab_in), custom_call_target="tpu_custom_call" | custom-call | tf_op jit(solution)/shard_map/pallas_call | solution.py:665

commit v4 on v3

--- a/solution.py
+++ b/solution.py
@@ -354,7 +354,6 @@
     barrier = pltpu.get_barrier_semaphore()
     for delta in partners:
         pl.semaphore_signal(barrier, inc=1, device_id=device(*delta), device_id_type=MESH)
-    pl.semaphore_wait(barrier, len(partners))
 
     copies = [
         pltpu.make_async_remote_copy(
@@ -365,8 +364,6 @@
     ]
     for load in loads:
         load.wait()
-    for copy in copies[:direct]:
-        copy.start()
     lane = lax.broadcasted_iota(jnp.int32, (rows, lanes), 1)
 
     def pack(plane, carry):
@@ -381,8 +378,13 @@
         return carry
 
     lax.fori_loop(0, planes, pack, 0)
-    for copy in copies[direct:]:
-        copy.start()
+    pl.semaphore_wait(barrier, len(partners))
+    def block(m):
+        return messages[m][0][:2] == (0, 0)
+
+    order = sorted(range(len(messages)), key=lambda m: (block(m), m < direct))
+    for m in order:
+        copies[m].start()
     load_base.wait()
     load_accum.wait()
 

time: 58.2 us -> 51.9 us (0.89)
  Pallas kernels: 57.5 us -> 51 us
    pallas_call x1, Pallas kernels: 55.4 us -> 48.9 us  [shards(): pl.pallas_call(functools.partial(section_kernel, sizes, groups), out_shap...]
where the time goes in v4:
time: 51.9 us; the launch traced here: 51.6 us
  Pallas kernels  51 us (98%)
  between operations  0.64 us (1%)
    pallas_call x1, Pallas kernels, shards(): pl.pallas_call(functools.partial(section_kernel, sizes, groups), out_shap...  48.9 us
    pallas_call x1, Pallas kernels, shards(): pl.pallas_call(put_out, out_shape=(block, block, slab), in_specs=[pl.Bloc...  2.05 us

profile of v4, /device:TPU:0, one launch (start us, length us, event | category | flops | bytes accessed | tf_op | source)
XLA Modules:
  0.0 51.6 jit_solution(4509550920546317119)
XLA Ops:
  0.6 48.9 %shard_map.58 = (f32[25,2,16,128]{3,2,1,0:T(8,128)S(1)}, f32[25,2,16,128]{3,2,1,0:T(8,128)S(1)}, f32[25,2,64,256]{3,2,1,0:T(8,128)S(1)}) custom-call(f32[25,2,16,128]{3,2,1,0:T(8,128)} %section.1, f32[25,2,16,128]{3,2,1,0:T(8,128)} %base.1, f32[25,2,16,128]{3,2,1,0:T(8,128)} %accum.1), custom_call_target="tpu_custom_call" | custom-call | tf_op jit(solution)/shard_map/pallas_call | solution.py:648
  49.6 2.1 %shard_map.59 = (f32[25,2,16,128]{3,2,1,0:T(8,128)}, f32[25,2,16,128]{3,2,1,0:T(8,128)}, f32[25,2,64,256]{3,2,1,0:T(8,128)}) custom-call(f32[25,2,16,128]{3,2,1,0:T(8,128)S(1)} %get-tuple-element.6.ns_in, f32[25,2,16,128]{3,2,1,0:T(8,128)S(1)} %get-tuple-element.7.na_in, f32[25,2,64,256]{3,2,1,0:T(8,128)S(1)} %get-tuple-element.8.slab_in), custom_call_target="tpu_custom_call" | custom-call | tf_op jit(solution)/shard_map/pallas_call | solution.py:667
